TPU v7x, 128 devices: a whole 4x4x4 slice. The times are simulated.
128 devices in a mesh: dp: 8 (over x, z_hi), tp: 16 (over z_lo, y, core).
Axes of the slice: x: 4, y: 4, z: 4 (z_hi: 2, z_lo: 2; z = z_hi * 2 + z_lo), core: 2. Of those that a mesh axis runs over, the one named last changes fastest.
Arguments:
- hidden_in: bfloat16 [4, 64, 4096], P(None, 'dp'), may hold values from -6 to 6
- pre_gain: float32 [4096], replicated, may hold values from 0.25 to 1.75
- w_zx: bfloat16 [4096, 2, 8192], P(None, None, 'tp'), may hold values from -0.09375 to 0.09375
- zx_codes: bfloat16 [4096, 2, 8192], P(('dp', 'tp')), may hold values from -4 to 4
- zx_exponents: int32 [32, 2, 64], P('dp', None, 'tp'), may hold values from -9 to -6
- w_bc: bfloat16 [4096, 2048], P(None, 'tp'), may hold values from -0.09375 to 0.09375
- w_dt: bfloat16 [4096, 128], P(None, 'tp'), may hold values from -0.09375 to 0.09375
- conv_x: float32 [5, 8192], P(None, 'tp'), may hold values from -0.6 to 0.6
- conv_bc: float32 [5, 2048], P(None, 'tp'), may hold values from -0.6 to 0.6
- dt_bias: float32 [128], P('tp'), may hold values from -2 to 0.5
- decay_rate: float32 [128], P('tp'), may hold values from 0.05 to 2
- skip_gain: float32 [128], P('tp'), may hold values from 0.5 to 1.5
- conv_state_x: bfloat16 [64, 3, 8192], P('dp', None, 'tp'), may hold values from -6 to 6
- conv_state_bc: bfloat16 [64, 3, 2048], P('dp', None, 'tp'), may hold values from -6 to 6
- ssm_state: float32 [64, 128, 64, 256], P('dp', 'tp'), may hold values from -6 to 6
- norm_gain: float32 [8192], P('tp'), may hold values from 0.25 to 1.75
- w_out: bfloat16 [8192, 4096], P('tp'), may hold values from -0.0625 to 0.0625
- out_codes: bfloat16 [8192, 4096], P('tp', 'dp'), may hold values from -4 to 4
- out_exponents: int32 [64, 32], P('tp', 'dp'), may hold values from -7 to -4
Outputs:
- mixed: bfloat16 [4, 64, 4096], P(None, 'dp', 'tp')
- final_state: float32 [64, 128, 64, 256], P('dp', 'tp')
All inputs are finite; a program needn't handle non-finite values.
Results may differ from a plain program's by a relative error of at most 0.014.
Values may be sent and summed in bfloat16 or wider, within the bound.
No kernel may reach another device: no remote copies, remote signals or barrier semaphores. Data moves between devices by JAX's collectives and lax.ppermute only.
A program may use at most 128 MiB of HBM per device.

v0:
```python
import jax
import jax.numpy as jnp
from jax import lax
from jax.sharding import PartitionSpec as P

H = 128
G = 4
BLK = 128
STEPS = 4
DI = 8192
EPS = 1e-05


def joined_along(tiles, dim):
    lengths = list(tiles.shape[1:])
    lengths[dim] *= tiles.shape[0]
    return jnp.moveaxis(tiles, 0, dim).reshape(lengths)


def copy_for_each(value, axis):
    devices = lax.axis_size(axis)
    return lax.all_to_all(
        jnp.broadcast_to(value[None], (devices, *value.shape)), axis, 0, 0, tiled=True
    )


def gather_directly(value, axis, dim):
    return joined_along(copy_for_each(value, axis), dim)


def cut_along(value, dim, devices):
    before, after = (value.shape[:dim], value.shape[dim + 1 :])
    return jnp.moveaxis(value.reshape(*before, devices, -1, *after), dim, 0)


def sent_and_summed(value, axis, dim):
    devices = lax.axis_size(axis)
    tiles = lax.all_to_all(cut_along(value, dim, devices), axis, 0, 0, tiled=True)
    return jnp.sum(tiles, axis=0)


def of_everyone(value, axis):
    return copy_for_each(value, axis).sum(axis=0)


def decode_pairs(codes, exponents, block):
    rows, pair, cols = codes.shape
    blocked = codes.astype(jnp.float32).reshape(rows // block, block, pair, cols // block, block)
    scales = jnp.exp2(exponents.astype(jnp.float32))
    return (blocked * scales[:, None, :, :, None]).reshape(rows, pair, cols)


def decode_matrix(codes, exponents, block):
    rows, cols = codes.shape
    blocked = codes.astype(jnp.float32).reshape(rows // block, block, cols // block, block)
    scales = jnp.exp2(exponents.astype(jnp.float32))
    return (blocked * scales[:, None, :, None]).reshape(rows, cols)


def conv_step(history, fresh, params):
    window = jnp.concatenate([history, fresh[:, None, :]], axis=1)
    mixed = jnp.sum(window * params[:4][None], axis=1) + params[4]
    return (jax.nn.silu(mixed), window[:, 1:])


def body(
    hidden_in,
    pre_gain,
    w_zx,
    zx_codes,
    zx_exponents,
    w_bc,
    w_dt,
    conv_x,
    conv_bc,
    dt_bias,
    decay_rate,
    skip_gain,
    conv_state_x,
    conv_state_bc,
    ssm_state,
    norm_gain,
    w_out,
    out_codes,
    out_exponents,
):
    replica = lax.axis_index("dp")
    slot = lax.axis_index("tp")
    traded = lax.all_to_all(zx_codes, "tp", split_axis=2, concat_axis=0, tiled=True)
    zx_delta = decode_pairs(traded, zx_exponents, BLK)
    row_span = traded.shape[0]
    local_cols = traded.shape[2]
    w_rows = lax.dynamic_slice_in_dim(w_zx, replica * row_span, row_span, 0)
    zx_weights = (
        (w_rows.astype(jnp.float32) + zx_delta)
        .astype(jnp.bfloat16)
        .reshape(row_span, 2 * local_cols)
    )
    out_piece = decode_matrix(out_codes, out_exponents, BLK).astype(jnp.bfloat16)
    out_full = lax.all_gather(out_piece, "dp", axis=1, tiled=True)
    new_out = (w_out.astype(jnp.float32) + out_full.astype(jnp.float32)).astype(jnp.bfloat16)
    heads_here = ssm_state.shape[1]
    states_n = ssm_state.shape[3]
    group = slot * heads_here // (H // G)
    group_mask = (jnp.arange(G) == group).astype(jnp.float32)
    history_x = conv_state_x.astype(jnp.float32)
    history_bc = conv_state_bc.astype(jnp.float32)
    state = ssm_state
    results = []
    carried = None
    for step in range(STEPS):
        x = hidden_in[step].astype(jnp.float32)
        if step > 0:
            x = x + carried.astype(jnp.float32)
        rows = x.shape[0]
        normed = (x * lax.rsqrt(jnp.mean(x * x, -1, keepdims=True) + EPS) * pre_gain).astype(
            jnp.bfloat16
        )
        everyone = gather_directly(normed, "dp", 0)
        own_cols = lax.dynamic_slice_in_dim(everyone, replica * row_span, row_span, 1)
        zx = sent_and_summed(
            jnp.dot(own_cols, zx_weights, preferred_element_type=jnp.float32), "dp", 0
        )
        zx = zx.reshape(rows, 2, local_cols)
        gate = zx[:, 0]
        inner = zx[:, 1]
        bc_raw = jnp.dot(normed, w_bc, preferred_element_type=jnp.float32)
        dt_raw = jnp.dot(normed, w_dt, preferred_element_type=jnp.float32)
        conv_inner, history_x = conv_step(history_x, inner, conv_x)
        conv_piece, history_bc = conv_step(history_bc, bc_raw, conv_bc)
        bc_all = gather_directly(conv_piece, "tp", 1)
        b_group = lax.dynamic_slice_in_dim(bc_all, group * states_n, states_n, 1)
        c_group = lax.dynamic_slice_in_dim(bc_all, G * states_n + group * states_n, states_n, 1)
        step_size = jax.nn.softplus(dt_raw + dt_bias)
        decay = jnp.exp(-step_size * decay_rate)
        inner_heads = conv_inner.reshape(rows, heads_here, -1)
        state = (
            decay[:, :, None, None] * state
            + (step_size[:, :, None] * inner_heads)[:, :, :, None] * b_group[:, None, None, :]
        )
        read = (
            jnp.einsum("rhpn,rn->rhp", state, c_group, precision=lax.Precision.HIGHEST)
            + skip_gain[:, None] * inner_heads
        )
        gated = read.reshape(rows, local_cols) * jax.nn.silu(gate)
        squares = jnp.sum(gated * gated, -1)
        totals = of_everyone(squares[:, None] * group_mask, "tp")
        mean_sq = jnp.sum(totals * group_mask, -1) / (DI // G)
        scaled = (gated * lax.rsqrt(mean_sq + EPS)[:, None] * norm_gain).astype(jnp.bfloat16)
        partial_value = jnp.dot(scaled, new_out, preferred_element_type=jnp.float32)
        summed = sent_and_summed(partial_value, "tp", 1).astype(jnp.bfloat16)
        results.append(summed)
        if step + 1 < STEPS:
            carried = gather_directly(summed, "tp", 1)
    return (jnp.stack(results), state)


def solution(mesh):
    return jax.shard_map(
        body,
        mesh=mesh,
        in_specs=(
            P(None, "dp", None),
            P(),
            P(None, None, "tp"),
            P(("dp", "tp"), None, None),
            P("dp", None, "tp"),
            P(None, "tp"),
            P(None, "tp"),
            P(None, "tp"),
            P(None, "tp"),
            P("tp"),
            P("tp"),
            P("tp"),
            P("dp", None, "tp"),
            P("dp", None, "tp"),
            P("dp", "tp", None, None),
            P("tp"),
            P("tp", None),
            P("tp", "dp"),
            P("tp", "dp"),
        ),
        out_specs=(P(None, "dp", "tp"), P("dp", "tp", None, None)),
        check_vma=False,
    )
```

profile of v0, /device:TPU:1, one launch (start us, length us, event | category | flops | bytes accessed | tf_op | source)
XLA Modules:
  0.0 413.4 jit_solution(10557720529095760822)
XLA Ops:
  10.4 7.4 %copy.32 = bf16[32,2,8192]{0,1,2:T(2,128)(2,1)} copy(bf16[32,2,8192]{2,1,0:T(2,128)(2,1)S(1)} %copy-done.4) | data formatting | bytes 2097152 | tf_op args[3]
  17.8 10.0 %reshape.669 = bf16[16,2,16384]{2,1,0:T(2,128)(2,1)} reshape(bf16[8192,2,32]{2,1,0:T(2,128)(2,1)} %bitcast.196) | data formatting | bytes 2097152
  27.8 7.3 %all-to-all-start.1 = ((bf16[16,2,16384]{2,1,0:T(2,128)(2,1)}), bf16[16,2,16384]{2,1,0:T(2,128)(2,1)S(1)}, u32[]{:S(2)}, u32[]{:S(2)}) async-start(bf16[16,2,16384]{2,1,0:T(2,128)(2,1)} %reshape.669), calls=%async_computation.1 | async-start | bytes 2097152 | tf_op jit(solution)/shard_map/all_to_all | solution.py:89
  42.1 8.8 %all-to-all-done.1 = bf16[16,2,16384]{2,1,0:T(2,128)(2,1)S(1)} async-done(((bf16[16,2,16384]{2,1,0:T(2,128)(2,1)}), bf16[16,2,16384]{2,1,0:T(2,128)(2,1)S(1)}, u32[]{:S(2)}, u32[]{:S(2)}) %all-to-all-start.1) | async-done | bytes 1048608 | tf_op jit(solution)/shard_map/all_to_all | solution.py:89
  51.7 7.0 %all-to-all-start = ((bf16[8,8,4096]{2,1,0:T(8,128)(2,1)}), bf16[8,8,4096]{2,1,0:T(8,128)(2,1)}, u32[]{:S(2)}, u32[]{:S(2)}) async-start(bf16[8,8,4096]{2,1,0:T(8,128)(2,1)} %broadcast_in_dim.47), calls=%async_computation | async-start | bytes 1048576 | tf_op jit(solution)/shard_map/all_to_all | solution.py:22
  62.2 8.9 %convert_bitcast_fusion = f32[16,32,2,512]{1,2,3,0:T(2,128)} fusion(bf16[32,2,16,512]{0,1,3,2:T(2,128)(2,1)} %bitcast.195), kind=kLoop, calls=%fused_computation | loop fusion | flops 524288 | bytes 3145728 | tf_op jit(solution)/shard_map/convert_element_type | solution.py:48
  71.1 11.6 %copy.33 = f32[16,32,2,512]{3,2,1,0:T(2,128)} copy(f32[16,32,2,512]{1,2,3,0:T(2,128)} %convert_bitcast_fusion) | data formatting | bytes 4194304 | tf_op jit(solution)/shard_map/convert_element_type | solution.py:48
  98.4 6.9 %all-to-all-start.2 = ((f32[8,8,1024]{2,1,0:T(8,128)}), f32[8,8,1024]{2,1,0:T(8,128)S(1)}, u32[]{:S(2)}, u32[]{:S(2)}) async-start(f32[8,8,1024]{2,1,0:T(8,128)} %fusion.49), calls=%async_computation.2 | async-start | bytes 524288 | tf_op jit(solution)/shard_map/all_to_all | solution.py:38
  113.7 7.6 %fusion.1 = f32[8,1,8,64]{3,1,2,0:T(1,128)S(1)} fusion(f32[8,8,64,256]{3,2,1,0:T(8,128)} %param.33, f32[8,256]{1,0:T(8,128)S(1)} %get-tuple-element.17, f32[8,8,64]{2,1,0:T(8,128)S(1)} %broadcast_multiply_fusion.3, f32[8,8]{1,0:T(8,128)S(1)} %get-tuple-element.26, f32[8,256,1,1]{1,0,2,3:T(8,128)S(1)} %get-tuple-element.16), kind=kOutput, calls=%fused_computation.7 | convolution fusion | flops 15728640 | bytes 4243712 | tf_op jit(solution)/shard_map/rhpn,rn->rhp/dot_general | solution.py:142
  133.7 7.3 %fusion = bf16[4096,512]{0,1:T(8,128)(2,1)} fusion(bf16[512,4096]{1,0:T(8,128)(2,1)} %all-gather.2.cloned.1.call-done, bf16[512,4096]{1,0:T(8,128)(2,1)} %param.35), kind=kLoop, calls=%fused_computation.2 | loop fusion | flops 8388608 | bytes 12582912 | tf_op jit(solution)/shard_map/dot_general | solution.py:150
  141.0 6.5 %copy.46 = bf16[4096,512]{1,0:T(8,128)(2,1)} copy(bf16[4096,512]{0,1:T(8,128)(2,1)} %fusion) | data formatting | bytes 8388608 | tf_op jit(solution)/shard_map/dot_general | solution.py:150
  176.8 10.2 %all-to-all-done.7 = bf16[8,8,4096]{2,1,0:T(8,128)(2,1)S(1)} async-done(((bf16[8,8,4096]{2,1,0:T(8,128)(2,1)}), bf16[8,8,4096]{2,1,0:T(8,128)(2,1)S(1)}, u32[]{:S(2)}, u32[]{:S(2)}) %all-to-all-start.7) | async-done | bytes 524320 | tf_op jit(solution)/shard_map/all_to_all | solution.py:22
  201.6 7.2 %all-to-all-done.8 = f32[8,8,1024]{2,1,0:T(8,128)S(1)} async-done(((f32[8,8,1024]{2,1,0:T(8,128)}), f32[8,8,1024]{2,1,0:T(8,128)S(1)}, u32[]{:S(2)}, u32[]{:S(2)}) %all-to-all-start.8) | async-done | bytes 262176 | tf_op jit(solution)/shard_map/all_to_all | solution.py:38
  209.1 7.6 %fusion.11 = f32[8,1,8,64]{3,1,2,0:T(1,128)S(1)} fusion(f32[8,8,64,256]{3,2,1,0:T(8,128)} %param.33, f32[8,256]{1,0:T(8,128)S(1)} %get-tuple-element.15, f32[8,8,64]{2,1,0:T(8,128)S(1)} %broadcast_multiply_fusion.2, f32[8,8]{1,0:T(8,128)S(1)} %get-tuple-element.28, f32[8,256]{1,0:T(8,128)S(1)} %get-tuple-element.17, ...), kind=kOutput, calls=%fused_computation.22 | convolution fusion | flops 18874368 | bytes 4268544 | tf_op jit(solution)/shard_map/rhpn,rn->rhp/dot_general | solution.py:142
  217.0 10.2 %all_to_all.124 = f32[16,8,4]{1,2,0:T(4,128)S(1)} all-to-all(f32[16,8,4]{1,2,0:T(4,128)S(1)} %broadcast_in_dim.56), channel_id=1, replica_groups=mesh['dp'=8,'tp'=16] {'tp'}, dimensions={0} | all-to-all | bytes 4096 | tf_op jit(solution)/shard_map/all_to_all | solution.py:22
  256.7 10.4 %all-to-all-done.13 = bf16[8,8,4096]{2,1,0:T(8,128)(2,1)S(1)} async-done(((bf16[8,8,4096]{2,1,0:T(8,128)(2,1)}), bf16[8,8,4096]{2,1,0:T(8,128)(2,1)S(1)}, u32[]{:S(2)}, u32[]{:S(2)}) %all-to-all-start.13) | async-done | bytes 524320 | tf_op jit(solution)/shard_map/all_to_all | solution.py:22
  281.7 7.4 %all-to-all-done.14 = f32[8,8,1024]{2,1,0:T(8,128)S(1)} async-done(((f32[8,8,1024]{2,1,0:T(8,128)}), f32[8,8,1024]{2,1,0:T(8,128)S(1)}, u32[]{:S(2)}, u32[]{:S(2)}) %all-to-all-start.14) | async-done | bytes 262176 | tf_op jit(solution)/shard_map/all_to_all | solution.py:38
  289.3 8.0 %fusion.2 = f32[8,1,8,64]{3,1,2,0:T(1,128)S(1)} fusion(f32[8,256]{1,0:T(8,128)S(1)} %get-tuple-element.13, f32[8,8,64]{2,1,0:T(8,128)S(1)} %broadcast_multiply_fusion.1, f32[8,8]{1,0:T(8,128)S(1)} %get-tuple-element.30, f32[8,8,64,256]{3,2,1,0:T(8,128)} %param.33, f32[8,256]{1,0:T(8,128)S(1)} %get-tuple-element.15, ...), kind=kOutput, calls=%fused_computation.8 | convolution fusion | flops 22020096 | bytes 4293376 | tf_op jit(solution)/shard_map/rhpn,rn->rhp/dot_general | solution.py:142
  297.6 10.0 %all_to_all.125 = f32[16,8,4]{1,2,0:T(4,128)S(1)} all-to-all(f32[16,8,4]{1,2,0:T(4,128)S(1)} %broadcast_in_dim.62), channel_id=1, replica_groups=mesh['dp'=8,'tp'=16] {'tp'}, dimensions={0} | all-to-all | bytes 4096 | tf_op jit(solution)/shard_map/all_to_all | solution.py:22
  337.2 10.4 %all-to-all-done.19 = bf16[8,8,4096]{2,1,0:T(8,128)(2,1)S(1)} async-done(((bf16[8,8,4096]{2,1,0:T(8,128)(2,1)}), bf16[8,8,4096]{2,1,0:T(8,128)(2,1)S(1)}, u32[]{:S(2)}, u32[]{:S(2)}) %all-to-all-start.19) | async-done | bytes 524320 | tf_op jit(solution)/shard_map/all_to_all | solution.py:22
  362.1 7.4 %all-to-all-done.20 = f32[8,8,1024]{2,1,0:T(8,128)S(1)} async-done(((f32[8,8,1024]{2,1,0:T(8,128)}), f32[8,8,1024]{2,1,0:T(8,128)S(1)}, u32[]{:S(2)}, u32[]{:S(2)}) %all-to-all-start.20) | async-done | bytes 262176 | tf_op jit(solution)/shard_map/all_to_all | solution.py:38
  369.8 6.2 %multiply_add_fusion = f32[8,8,64,256]{3,2,1,0:T(8,128)S(1)} fusion(f32[8,256]{1,0:T(8,128)S(1)} %get-tuple-element.11, f32[8,8,64]{2,1,0:T(8,128)S(1)} %broadcast_multiply_fusion, f32[8,8]{1,0:T(8,128)S(1)} %get-tuple-element.32, f32[8,256]{1,0:T(8,128)S(1)} %get-tuple-element.13, f32[8,8,64]{2,1,0:T(8,128)S(1)} %broadcast_multiply_fusion.1, ...), kind=kLoop, calls=%fused_computation.3 | loop fusion | flops 12582912 | bytes 8487936 | tf_op jit(solution)/shard_map/add | solution.py:138
  383.3 10.0 %all_to_all.126 = f32[16,8,4]{1,2,0:T(4,128)S(1)} all-to-all(f32[16,8,4]{1,2,0:T(4,128)S(1)} %broadcast_in_dim.68), channel_id=1, replica_groups=mesh['dp'=8,'tp'=16] {'tp'}, dimensions={0} | all-to-all | bytes 4096 | tf_op jit(solution)/shard_map/all_to_all | solution.py:22
  397.0 8.9 %all_to_all.127 = f32[16,8,256]{2,1,0:T(8,128)S(1)} all-to-all(f32[16,8,256]{2,1,0:T(8,128)S(1)} %convolution_bitcast_fusion), channel_id=1, replica_groups=mesh['dp'=8,'tp'=16] {'tp'}, dimensions={0} | all-to-all | bytes 262144 | tf_op jit(solution)/shard_map/all_to_all | solution.py:38
  (206 shorter events, 195.5 us)
Async XLA Ops:
  7.2 126.6 %all-gather.2.cloned.1.call-start = ((), (), s32[]{:S(2)}) async-start(), calls=%async_computation.24 | async-start | bytes 4718592 | tf_op jit(solution)/shard_map/all_gather | solution.py:100
  27.8 23.1 %all-to-all-start.1 = ((bf16[16,2,16384]{2,1,0:T(2,128)(2,1)}), bf16[16,2,16384]{2,1,0:T(2,128)(2,1)S(1)}, u32[]{:S(2)}, u32[]{:S(2)}) async-start(bf16[16,2,16384]{2,1,0:T(2,128)(2,1)} %reshape.669), calls=%async_computation.1 | async-start | bytes 2097152 | tf_op jit(solution)/shard_map/all_to_all | solution.py:89
  51.7 35.9 %all-to-all-start = ((bf16[8,8,4096]{2,1,0:T(8,128)(2,1)}), bf16[8,8,4096]{2,1,0:T(8,128)(2,1)}, u32[]{:S(2)}, u32[]{:S(2)}) async-start(bf16[8,8,4096]{2,1,0:T(8,128)(2,1)} %broadcast_in_dim.47), calls=%async_computation | async-start | bytes 1048576 | tf_op jit(solution)/shard_map/all_to_all | solution.py:22
  86.8 34.5 %copy-start.7 = (f32[8]{0:T(128)S(1)}, f32[8]{0:T(128)}, u32[]{:S(2)}) copy-start(f32[8]{0:T(128)} %param.30) | copy-start | bytes 100
  87.6 40.0 %copy-start.13 = (f32[512]{0:T(512)S(1)}, f32[512]{0:T(512)}, u32[]{:S(2)}) copy-start(f32[512]{0:T(512)} %param.34) | copy-start | bytes 6148
  88.2 10.2 %all-to-all-start.3 = ((f32[16,8,128]{2,1,0:T(8,128)}), f32[16,8,128]{2,1,0:T(8,128)S(1)}, u32[]{:S(2)}, u32[]{:S(2)}) async-start(f32[16,8,128]{2,1,0:T(8,128)} %broadcast_in_dim.49), calls=%async_computation.3 | async-start | bytes 131072 | tf_op jit(solution)/shard_map/all_to_all | solution.py:22
  98.4 14.3 %all-to-all-start.2 = ((f32[8,8,1024]{2,1,0:T(8,128)}), f32[8,8,1024]{2,1,0:T(8,128)S(1)}, u32[]{:S(2)}, u32[]{:S(2)}) async-start(f32[8,8,1024]{2,1,0:T(8,128)} %fusion.49), calls=%async_computation.2 | async-start | bytes 524288 | tf_op jit(solution)/shard_map/all_to_all | solution.py:38
  122.3 11.2 %all-to-all-start.4 = ((f32[16,8,4]{1,2,0:T(4,128)}), f32[16,8,4]{1,2,0:T(4,128)S(1)}, u32[]{:S(2)}, u32[]{:S(2)}) async-start(f32[16,8,4]{1,2,0:T(4,128)} %broadcast_in_dim.50), calls=%async_computation.4 | async-start | bytes 65536 | tf_op jit(solution)/shard_map/all_to_all | solution.py:22
  151.5 49.9 %copy-start.11 = (f32[8]{0:T(128)S(1)}, f32[8]{0:T(128)}, u32[]{:S(2)}) copy-start(f32[8]{0:T(128)} %param.28) | copy-start | bytes 100
  151.5 10.0 %all-to-all-start.5 = ((f32[16,8,256]{2,1,0:T(8,128)}), f32[16,8,256]{2,1,0:T(8,128)S(1)}, u32[]{:S(2)}, u32[]{:S(2)}) async-start(f32[16,8,256]{2,1,0:T(8,128)} %convolution_bitcast_fusion.3), calls=%async_computation.5 | async-start | bytes 262144 | tf_op jit(solution)/shard_map/all_to_all | solution.py:38
  162.1 9.7 %all-to-all-start.6 = ((bf16[16,8,256]{2,1,0:T(8,128)(2,1)}), bf16[16,8,256]{2,1,0:T(8,128)(2,1)S(1)}, u32[]{:S(2)}, u32[]{:S(2)}) async-start(bf16[16,8,256]{2,1,0:T(8,128)(2,1)} %broadcast_in_dim.51), calls=%async_computation.6 | async-start | bytes 131072 | tf_op jit(solution)/shard_map/all_to_all | solution.py:22
  173.0 14.0 %all-to-all-start.7 = ((bf16[8,8,4096]{2,1,0:T(8,128)(2,1)}), bf16[8,8,4096]{2,1,0:T(8,128)(2,1)S(1)}, u32[]{:S(2)}, u32[]{:S(2)}) async-start(bf16[8,8,4096]{2,1,0:T(8,128)(2,1)} %broadcast_in_dim.53), calls=%async_computation.7 | async-start | bytes 1048576 | tf_op jit(solution)/shard_map/all_to_all | solution.py:22
  187.7 10.3 %all-to-all-start.9 = ((f32[16,8,128]{2,1,0:T(8,128)}), f32[16,8,128]{2,1,0:T(8,128)S(1)}, u32[]{:S(2)}, u32[]{:S(2)}) async-start(f32[16,8,128]{2,1,0:T(8,128)} %broadcast_in_dim.55), calls=%async_computation.9 | async-start | bytes 131072 | tf_op jit(solution)/shard_map/all_to_all | solution.py:22
  198.0 10.8 %all-to-all-start.8 = ((f32[8,8,1024]{2,1,0:T(8,128)}), f32[8,8,1024]{2,1,0:T(8,128)S(1)}, u32[]{:S(2)}, u32[]{:S(2)}) async-start(f32[8,8,1024]{2,1,0:T(8,128)} %fusion.47), calls=%async_computation.8 | async-start | bytes 524288 | tf_op jit(solution)/shard_map/all_to_all | solution.py:38
  231.6 9.8 %all-to-all-start.11 = ((f32[16,8,256]{2,1,0:T(8,128)}), f32[16,8,256]{2,1,0:T(8,128)S(1)}, u32[]{:S(2)}, u32[]{:S(2)}) async-start(f32[16,8,256]{2,1,0:T(8,128)} %convolution_bitcast_fusion.2), calls=%async_computation.11 | async-start | bytes 262144 | tf_op jit(solution)/shard_map/all_to_all | solution.py:38
  242.0 9.7 %all-to-all-start.12 = ((bf16[16,8,256]{2,1,0:T(8,128)(2,1)}), bf16[16,8,256]{2,1,0:T(8,128)(2,1)S(1)}, u32[]{:S(2)}, u32[]{:S(2)}) async-start(bf16[16,8,256]{2,1,0:T(8,128)(2,1)} %broadcast_in_dim.57), calls=%async_computation.12 | async-start | bytes 131072 | tf_op jit(solution)/shard_map/all_to_all | solution.py:22
  253.0 14.2 %all-to-all-start.13 = ((bf16[8,8,4096]{2,1,0:T(8,128)(2,1)}), bf16[8,8,4096]{2,1,0:T(8,128)(2,1)S(1)}, u32[]{:S(2)}, u32[]{:S(2)}) async-start(bf16[8,8,4096]{2,1,0:T(8,128)(2,1)} %broadcast_in_dim.59), calls=%async_computation.13 | async-start | bytes 1048576 | tf_op jit(solution)/shard_map/all_to_all | solution.py:22
  267.8 10.3 %all-to-all-start.15 = ((f32[16,8,128]{2,1,0:T(8,128)}), f32[16,8,128]{2,1,0:T(8,128)S(1)}, u32[]{:S(2)}, u32[]{:S(2)}) async-start(f32[16,8,128]{2,1,0:T(8,128)} %broadcast_in_dim.61), calls=%async_computation.15 | async-start | bytes 131072 | tf_op jit(solution)/shard_map/all_to_all | solution.py:22
  278.1 11.0 %all-to-all-start.14 = ((f32[8,8,1024]{2,1,0:T(8,128)}), f32[8,8,1024]{2,1,0:T(8,128)S(1)}, u32[]{:S(2)}, u32[]{:S(2)}) async-start(f32[8,8,1024]{2,1,0:T(8,128)} %fusion.45), calls=%async_computation.14 | async-start | bytes 524288 | tf_op jit(solution)/shard_map/all_to_all | solution.py:38
  312.0 9.8 %all-to-all-start.17 = ((f32[16,8,256]{2,1,0:T(8,128)}), f32[16,8,256]{2,1,0:T(8,128)S(1)}, u32[]{:S(2)}, u32[]{:S(2)}) async-start(f32[16,8,256]{2,1,0:T(8,128)} %convolution_bitcast_fusion.1), calls=%async_computation.17 | async-start | bytes 262144 | tf_op jit(solution)/shard_map/all_to_all | solution.py:38
  322.5 9.7 %all-to-all-start.18 = ((bf16[16,8,256]{2,1,0:T(8,128)(2,1)}), bf16[16,8,256]{2,1,0:T(8,128)(2,1)S(1)}, u32[]{:S(2)}, u32[]{:S(2)}) async-start(bf16[16,8,256]{2,1,0:T(8,128)(2,1)} %broadcast_in_dim.63), calls=%async_computation.18 | async-start | bytes 131072 | tf_op jit(solution)/shard_map/all_to_all | solution.py:22
  333.4 14.2 %all-to-all-start.19 = ((bf16[8,8,4096]{2,1,0:T(8,128)(2,1)}), bf16[8,8,4096]{2,1,0:T(8,128)(2,1)S(1)}, u32[]{:S(2)}, u32[]{:S(2)}) async-start(bf16[8,8,4096]{2,1,0:T(8,128)(2,1)} %broadcast_in_dim.65), calls=%async_computation.19 | async-start | bytes 1048576 | tf_op jit(solution)/shard_map/all_to_all | solution.py:22
  348.2 10.3 %all-to-all-start.21 = ((f32[16,8,128]{2,1,0:T(8,128)}), f32[16,8,128]{2,1,0:T(8,128)S(1)}, u32[]{:S(2)}, u32[]{:S(2)}) async-start(f32[16,8,128]{2,1,0:T(8,128)} %broadcast_in_dim.67), calls=%async_computation.21 | async-start | bytes 131072 | tf_op jit(solution)/shard_map/all_to_all | solution.py:22
  358.5 11.0 %all-to-all-start.20 = ((f32[8,8,1024]{2,1,0:T(8,128)}), f32[8,8,1024]{2,1,0:T(8,128)S(1)}, u32[]{:S(2)}, u32[]{:S(2)}) async-start(f32[8,8,1024]{2,1,0:T(8,128)} %fusion.43), calls=%async_computation.20 | async-start | bytes 524288 | tf_op jit(solution)/shard_map/all_to_all | solution.py:38
  (12 other events, 199.7 us)
Sparse Core Ops, SparseCore 0:
  10.5 86.1 all-gather.1
where the time goes:
time: 416 us; the launch traced here: 413 us
  waiting for transfers between devices  128 us (31%)
  starting transfers between devices  87.5 us (21%)
  local copies, waits for them, and re-layouts  58.5 us (14%)
  matrix products  50.9 us (12%)
  blocking collectives  39.2 us (9%)
  other arithmetic  34.5 us (8%)
  between operations  14.6 us (4%)
    all_to_all x12, waiting for transfers between devices, copy_for_each(): lax.all_to_all(jnp.broadcast_to(value[None], (devices, *value.shape)), ax...  73.2 us
    all_to_all x12, starting transfers between devices, copy_for_each(): lax.all_to_all(jnp.broadcast_to(value[None], (devices, *value.shape)), ax...  51.8 us
    all_to_all x7, waiting for transfers between devices, sent_and_summed(): lax.all_to_all(cut_along(value, dim, devices), axis, 0, 0, tiled=True)  46.2 us
    all_to_all x3, blocking collectives, copy_for_each(): lax.all_to_all(jnp.broadcast_to(value[None], (devices, *value.shape)), ax...  30.2 us
    all_to_all x7, starting transfers between devices, sent_and_summed(): lax.all_to_all(cut_along(value, dim, devices), axis, 0, 0, tiled=True)  28.3 us
    dot_general x4, matrix products, body(): jnp.einsum('rhpn,rn->rhp', state, c_group, precision=lax.Precision.HIGHEST)  28.2 us
    unnamed x33, local copies, waits for them, and re-layouts  23 us
    dot_general x4, matrix products, body(): partial_value = jnp.dot(scaled, new_out, preferred_element_type=jnp.float32)  15.5 us
  transfers between devices with their start and end apart: 21, of which 19 were waited for; matrix products, arithmetic and copies ran while one was open for 17% of the time, Pallas kernels for 0%

commit v1 on v0

--- a/solution.py
+++ b/solution.py
@@ -86,7 +86,10 @@
 ):
     replica = lax.axis_index("dp")
     slot = lax.axis_index("tp")
-    traded = lax.all_to_all(zx_codes, "tp", split_axis=2, concat_axis=0, tiled=True)
+    peers = lax.axis_size("tp")
+    shards = jnp.stack(jnp.split(zx_codes, peers, axis=2), axis=0)
+    shards = lax.all_to_all(shards, "tp", split_axis=0, concat_axis=0)
+    traded = jnp.concatenate(shards, axis=0)
     zx_delta = decode_pairs(traded, zx_exponents, BLK)
     row_span = traded.shape[0]
     local_cols = traded.shape[2]

time: 416 us -> 396 us (0.952)
  local copies, waits for them, and re-layouts: 58.5 us -> 40.3 us
  other arithmetic: 34.5 us -> 24.9 us
  waiting for transfers between devices: 128 us -> 136 us
    convert_element_type x1 -> x0, local copies, waits for them, and re-layouts: 11.6 us -> none  [decode_pairs(): codes.astype(jnp.float32)]
    convert_element_type x1 -> x0, other arithmetic: 8.9 us -> none  [decode_pairs(): codes.astype(jnp.float32)]
    unnamed x33 -> x45, local copies, waits for them, and re-layouts: 23 us -> 15.6 us
    all_to_all x1, waiting for transfers between devices: 8.81 us -> 14.3 us  [body(): shards = lax.all_to_all(shards, 'tp', split_axis=0, concat_axis=0)]
  transfers between devices with their start and end apart: 21 -> 21, of which waited for: 19 -> 20; matrix products, arithmetic and copies ran while one was open for 17% -> 11% of each run, Pallas kernels for 0% -> 0%
where the time goes in v1:
time: 396 us; the launch traced here: 393 us
  waiting for transfers between devices  136 us (34%)
  starting transfers between devices  86.8 us (22%)
  matrix products  50.9 us (13%)
  local copies, waits for them, and re-layouts  40.3 us (10%)
  blocking collectives  39.4 us (10%)
  other arithmetic  24.9 us (6%)
  between operations  14.6 us (4%)
    all_to_all x12, waiting for transfers between devices, copy_for_each(): lax.all_to_all(jnp.broadcast_to(value[None], (devices, *value.shape)), ax...  73.9 us
    all_to_all x12, starting transfers between devices, copy_for_each(): lax.all_to_all(jnp.broadcast_to(value[None], (devices, *value.shape)), ax...  53.3 us
    all_to_all x7, waiting for transfers between devices, sent_and_summed(): lax.all_to_all(cut_along(value, dim, devices), axis, 0, 0, tiled=True)  48.3 us
    all_to_all x3, blocking collectives, copy_for_each(): lax.all_to_all(jnp.broadcast_to(value[None], (devices, *value.shape)), ax...  30.5 us
    dot_general x4, matrix products, body(): jnp.einsum('rhpn,rn->rhp', state, c_group, precision=lax.Precision.HIGHEST)  28.3 us
    all_to_all x7, starting transfers between devices, sent_and_summed(): lax.all_to_all(cut_along(value, dim, devices), axis, 0, 0, tiled=True)  26.1 us
    unnamed x45, local copies, waits for them, and re-layouts  15.6 us
    dot_general x4, matrix products, body(): partial_value = jnp.dot(scaled, new_out, preferred_element_type=jnp.float32)  15.5 us
  transfers between devices with their start and end apart: 21, of which 20 were waited for; matrix products, arithmetic and copies ran while one was open for 11% of the time, Pallas kernels for 0%

profile of v1, /device:TPU:1, one launch (start us, length us, event | category | flops | bytes accessed | tf_op | source)
XLA Modules:
  0.0 393.4 jit_solution(7191503117215772757)
XLA Ops:
  24.7 7.3 %all-to-all-start.1 = ((bf16[16,32,2,512]{3,2,1,0:T(2,128)(2,1)}), bf16[16,32,2,512]{3,2,1,0:T(2,128)(2,1)S(1)}, u32[]{:S(2)}, u32[]{:S(2)}) async-start(bf16[16,32,2,512]{3,2,1,0:T(2,128)(2,1)} %bitcast_dynamic-update-slice_fusion), calls=%async_computation.1 | async-start | bytes 2097152 | tf_op jit(solution)/shard_map/all_to_all | solution.py:91
  33.5 14.3 %all-to-all-done.1 = bf16[16,32,2,512]{3,2,1,0:T(2,128)(2,1)S(1)} async-done(((bf16[16,32,2,512]{3,2,1,0:T(2,128)(2,1)}), bf16[16,32,2,512]{3,2,1,0:T(2,128)(2,1)S(1)}, u32[]{:S(2)}, u32[]{:S(2)}) %all-to-all-start.1) | async-done | bytes 1048608 | tf_op jit(solution)/shard_map/all_to_all | solution.py:91
  48.6 7.0 %all-to-all-start = ((bf16[8,8,4096]{2,1,0:T(8,128)(2,1)}), bf16[8,8,4096]{2,1,0:T(8,128)(2,1)}, u32[]{:S(2)}, u32[]{:S(2)}) async-start(bf16[8,8,4096]{2,1,0:T(8,128)(2,1)} %broadcast_in_dim.47), calls=%async_computation | async-start | bytes 1048576 | tf_op jit(solution)/shard_map/all_to_all | solution.py:22
  66.6 6.0 %all-to-all-start.3 = ((f32[16,8,128]{2,1,0:T(8,128)}), f32[16,8,128]{2,1,0:T(8,128)S(1)}, u32[]{:S(2)}, u32[]{:S(2)}) async-start(f32[16,8,128]{2,1,0:T(8,128)} %broadcast_in_dim.49), calls=%async_computation.3 | async-start | bytes 131072 | tf_op jit(solution)/shard_map/all_to_all | solution.py:22
  84.6 8.0 %all-to-all-done.2 = f32[8,8,1024]{2,1,0:T(8,128)S(1)} async-done(((f32[8,8,1024]{2,1,0:T(8,128)}), f32[8,8,1024]{2,1,0:T(8,128)S(1)}, u32[]{:S(2)}, u32[]{:S(2)}) %all-to-all-start.2) | async-done | bytes 262176 | tf_op jit(solution)/shard_map/all_to_all | solution.py:38
  93.6 7.7 %fusion.1 = f32[8,1,8,64]{3,1,2,0:T(1,128)S(1)} fusion(f32[8,8,64,256]{3,2,1,0:T(8,128)} %param.33, f32[8,256]{1,0:T(8,128)S(1)} %get-tuple-element.17, f32[8,8,64]{2,1,0:T(8,128)S(1)} %broadcast_multiply_fusion.3, f32[8,8]{1,0:T(8,128)S(1)} %get-tuple-element.26, f32[8,256,1,1]{1,0,2,3:T(8,128)S(1)} %get-tuple-element.16), kind=kOutput, calls=%fused_computation.6 | convolution fusion | flops 15728640 | bytes 4243712 | tf_op jit(solution)/shard_map/rhpn,rn->rhp/dot_general | solution.py:145
  112.7 7.3 %fusion = bf16[4096,512]{0,1:T(8,128)(2,1)} fusion(bf16[512,4096]{1,0:T(8,128)(2,1)} %all-gather.2.cloned.1.call-done, bf16[512,4096]{1,0:T(8,128)(2,1)} %param.35), kind=kLoop, calls=%fused_computation.1 | loop fusion | flops 8388608 | bytes 12582912 | tf_op jit(solution)/shard_map/dot_general | solution.py:153
  120.0 6.5 %copy.37 = bf16[4096,512]{1,0:T(8,128)(2,1)} copy(bf16[4096,512]{0,1:T(8,128)(2,1)} %fusion) | data formatting | bytes 8388608 | tf_op jit(solution)/shard_map/dot_general | solution.py:153
  134.3 6.1 %all-to-all-done.5 = f32[16,8,256]{2,1,0:T(8,128)S(1)} async-done(((f32[16,8,256]{2,1,0:T(8,128)}), f32[16,8,256]{2,1,0:T(8,128)S(1)}, u32[]{:S(2)}, u32[]{:S(2)}) %all-to-all-start.5) | async-done | bytes 131104 | tf_op jit(solution)/shard_map/all_to_all | solution.py:38
  156.5 10.4 %all-to-all-done.7 = bf16[8,8,4096]{2,1,0:T(8,128)(2,1)S(1)} async-done(((bf16[8,8,4096]{2,1,0:T(8,128)(2,1)}), bf16[8,8,4096]{2,1,0:T(8,128)(2,1)S(1)}, u32[]{:S(2)}, u32[]{:S(2)}) %all-to-all-start.7) | async-done | bytes 524320 | tf_op jit(solution)/shard_map/all_to_all | solution.py:22
  181.5 7.3 %all-to-all-done.8 = f32[8,8,1024]{2,1,0:T(8,128)S(1)} async-done(((f32[8,8,1024]{2,1,0:T(8,128)}), f32[8,8,1024]{2,1,0:T(8,128)S(1)}, u32[]{:S(2)}, u32[]{:S(2)}) %all-to-all-start.8) | async-done | bytes 262176 | tf_op jit(solution)/shard_map/all_to_all | solution.py:38
  189.1 7.6 %fusion.11 = f32[8,1,8,64]{3,1,2,0:T(1,128)S(1)} fusion(f32[8,8,64,256]{3,2,1,0:T(8,128)} %param.33, f32[8,256]{1,0:T(8,128)S(1)} %get-tuple-element.15, f32[8,8,64]{2,1,0:T(8,128)S(1)} %broadcast_multiply_fusion.2, f32[8,8]{1,0:T(8,128)S(1)} %get-tuple-element.28, f32[8,256]{1,0:T(8,128)S(1)} %get-tuple-element.17, ...), kind=kOutput, calls=%fused_computation.21 | convolution fusion | flops 18874368 | bytes 4268544 | tf_op jit(solution)/shard_map/rhpn,rn->rhp/dot_general | solution.py:145
  197.0 10.1 %all_to_all.120 = f32[16,8,4]{1,2,0:T(4,128)S(1)} all-to-all(f32[16,8,4]{1,2,0:T(4,128)S(1)} %broadcast_in_dim.56), channel_id=1, replica_groups=mesh['dp'=8,'tp'=16] {'tp'}, dimensions={0} | all-to-all | bytes 4096 | tf_op jit(solution)/shard_map/all_to_all | solution.py:22
  215.1 6.1 %all-to-all-done.11 = f32[16,8,256]{2,1,0:T(8,128)S(1)} async-done(((f32[16,8,256]{2,1,0:T(8,128)}), f32[16,8,256]{2,1,0:T(8,128)S(1)}, u32[]{:S(2)}, u32[]{:S(2)}) %all-to-all-start.11) | async-done | bytes 131104 | tf_op jit(solution)/shard_map/all_to_all | solution.py:38
  236.6 10.4 %all-to-all-done.13 = bf16[8,8,4096]{2,1,0:T(8,128)(2,1)S(1)} async-done(((bf16[8,8,4096]{2,1,0:T(8,128)(2,1)}), bf16[8,8,4096]{2,1,0:T(8,128)(2,1)S(1)}, u32[]{:S(2)}, u32[]{:S(2)}) %all-to-all-start.13) | async-done | bytes 524320 | tf_op jit(solution)/shard_map/all_to_all | solution.py:22
  261.5 7.4 %all-to-all-done.14 = f32[8,8,1024]{2,1,0:T(8,128)S(1)} async-done(((f32[8,8,1024]{2,1,0:T(8,128)}), f32[8,8,1024]{2,1,0:T(8,128)S(1)}, u32[]{:S(2)}, u32[]{:S(2)}) %all-to-all-start.14) | async-done | bytes 262176 | tf_op jit(solution)/shard_map/all_to_all | solution.py:38
  269.2 8.0 %fusion.2 = f32[8,1,8,64]{3,1,2,0:T(1,128)S(1)} fusion(f32[8,256]{1,0:T(8,128)S(1)} %get-tuple-element.13, f32[8,8,64]{2,1,0:T(8,128)S(1)} %broadcast_multiply_fusion.1, f32[8,8]{1,0:T(8,128)S(1)} %get-tuple-element.30, f32[8,8,64,256]{3,2,1,0:T(8,128)} %param.33, f32[8,256]{1,0:T(8,128)S(1)} %get-tuple-element.15, ...), kind=kOutput, calls=%fused_computation.7 | convolution fusion | flops 22020096 | bytes 4293376 | tf_op jit(solution)/shard_map/rhpn,rn->rhp/dot_general | solution.py:145
  277.5 10.3 %all_to_all.121 = f32[16,8,4]{1,2,0:T(4,128)S(1)} all-to-all(f32[16,8,4]{1,2,0:T(4,128)S(1)} %broadcast_in_dim.62), channel_id=1, replica_groups=mesh['dp'=8,'tp'=16] {'tp'}, dimensions={0} | all-to-all | bytes 4096 | tf_op jit(solution)/shard_map/all_to_all | solution.py:22
  295.8 6.1 %all-to-all-done.17 = f32[16,8,256]{2,1,0:T(8,128)S(1)} async-done(((f32[16,8,256]{2,1,0:T(8,128)}), f32[16,8,256]{2,1,0:T(8,128)S(1)}, u32[]{:S(2)}, u32[]{:S(2)}) %all-to-all-start.17) | async-done | bytes 131104 | tf_op jit(solution)/shard_map/all_to_all | solution.py:38
  317.3 10.2 %all-to-all-done.19 = bf16[8,8,4096]{2,1,0:T(8,128)(2,1)S(1)} async-done(((bf16[8,8,4096]{2,1,0:T(8,128)(2,1)}), bf16[8,8,4096]{2,1,0:T(8,128)(2,1)S(1)}, u32[]{:S(2)}, u32[]{:S(2)}) %all-to-all-start.19) | async-done | bytes 524320 | tf_op jit(solution)/shard_map/all_to_all | solution.py:22
  342.1 7.2 %all-to-all-done.20 = f32[8,8,1024]{2,1,0:T(8,128)S(1)} async-done(((f32[8,8,1024]{2,1,0:T(8,128)}), f32[8,8,1024]{2,1,0:T(8,128)S(1)}, u32[]{:S(2)}, u32[]{:S(2)}) %all-to-all-start.20) | async-done | bytes 262176 | tf_op jit(solution)/shard_map/all_to_all | solution.py:38
  349.6 6.2 %multiply_add_fusion = f32[8,8,64,256]{3,2,1,0:T(8,128)S(1)} fusion(f32[8,256]{1,0:T(8,128)S(1)} %get-tuple-element.11, f32[8,8,64]{2,1,0:T(8,128)S(1)} %broadcast_multiply_fusion, f32[8,8]{1,0:T(8,128)S(1)} %get-tuple-element.32, f32[8,256]{1,0:T(8,128)S(1)} %get-tuple-element.13, f32[8,8,64]{2,1,0:T(8,128)S(1)} %broadcast_multiply_fusion.1, ...), kind=kLoop, calls=%fused_computation.2 | loop fusion | flops 12582912 | bytes 8487936 | tf_op jit(solution)/shard_map/add | solution.py:141
  363.1 10.2 %all_to_all.122 = f32[16,8,4]{1,2,0:T(4,128)S(1)} all-to-all(f32[16,8,4]{1,2,0:T(4,128)S(1)} %broadcast_in_dim.68), channel_id=1, replica_groups=mesh['dp'=8,'tp'=16] {'tp'}, dimensions={0} | all-to-all | bytes 4096 | tf_op jit(solution)/shard_map/all_to_all | solution.py:22
  377.0 8.9 %all_to_all.123 = f32[16,8,256]{2,1,0:T(8,128)S(1)} all-to-all(f32[16,8,256]{2,1,0:T(8,128)S(1)} %convolution_bitcast_fusion), channel_id=1, replica_groups=mesh['dp'=8,'tp'=16] {'tp'}, dimensions={0} | all-to-all | bytes 262144 | tf_op jit(solution)/shard_map/all_to_all | solution.py:38
  (217 shorter events, 182.2 us)
Async XLA Ops:
  7.2 105.5 %all-gather.2.cloned.1.call-start = ((), (), s32[]{:S(2)}) async-start(), calls=%async_computation.24 | async-start | bytes 4718592 | tf_op jit(solution)/shard_map/all_gather | solution.py:103
  10.4 45.2 %copy-start.12 = (s32[4,2,4]{2,1,0:T(2,128)S(1)}, s32[4,2,4]{2,1,0:T(2,128)}, u32[]{:S(2)}) copy-start(s32[4,2,4]{2,1,0:T(2,128)} %param.23) | copy-start | bytes 388
  24.7 23.1 %all-to-all-start.1 = ((bf16[16,32,2,512]{3,2,1,0:T(2,128)(2,1)}), bf16[16,32,2,512]{3,2,1,0:T(2,128)(2,1)S(1)}, u32[]{:S(2)}, u32[]{:S(2)}) async-start(bf16[16,32,2,512]{3,2,1,0:T(2,128)(2,1)} %bitcast_dynamic-update-slice_fusion), calls=%async_computation.1 | async-start | bytes 2097152 | tf_op jit(solution)/shard_map/all_to_all | solution.py:91
  48.6 17.3 %all-to-all-start = ((bf16[8,8,4096]{2,1,0:T(8,128)(2,1)}), bf16[8,8,4096]{2,1,0:T(8,128)(2,1)}, u32[]{:S(2)}, u32[]{:S(2)}) async-start(bf16[8,8,4096]{2,1,0:T(8,128)(2,1)} %broadcast_in_dim.47), calls=%async_computation | async-start | bytes 1048576 | tf_op jit(solution)/shard_map/all_to_all | solution.py:22
  65.2 41.4 %copy-start.13 = (f32[512]{0:T(512)S(1)}, f32[512]{0:T(512)}, u32[]{:S(2)}) copy-start(f32[512]{0:T(512)} %param.34) | copy-start | bytes 6148
  66.6 11.9 %all-to-all-start.3 = ((f32[16,8,128]{2,1,0:T(8,128)}), f32[16,8,128]{2,1,0:T(8,128)S(1)}, u32[]{:S(2)}, u32[]{:S(2)}) async-start(f32[16,8,128]{2,1,0:T(8,128)} %broadcast_in_dim.49), calls=%async_computation.3 | async-start | bytes 131072 | tf_op jit(solution)/shard_map/all_to_all | solution.py:22
  78.4 14.2 %all-to-all-start.2 = ((f32[8,8,1024]{2,1,0:T(8,128)}), f32[8,8,1024]{2,1,0:T(8,128)S(1)}, u32[]{:S(2)}, u32[]{:S(2)}) async-start(f32[8,8,1024]{2,1,0:T(8,128)} %fusion.49), calls=%async_computation.2 | async-start | bytes 524288 | tf_op jit(solution)/shard_map/all_to_all | solution.py:38
  102.2 10.3 %all-to-all-start.4 = ((f32[16,8,4]{1,2,0:T(4,128)}), f32[16,8,4]{1,2,0:T(4,128)S(1)}, u32[]{:S(2)}, u32[]{:S(2)}) async-start(f32[16,8,4]{1,2,0:T(4,128)} %broadcast_in_dim.50), calls=%async_computation.4 | async-start | bytes 65536 | tf_op jit(solution)/shard_map/all_to_all | solution.py:22
  130.5 50.8 %copy-start.11 = (f32[8]{0:T(128)S(1)}, f32[8]{0:T(128)}, u32[]{:S(2)}) copy-start(f32[8]{0:T(128)} %param.28) | copy-start | bytes 100
  130.5 10.0 %all-to-all-start.5 = ((f32[16,8,256]{2,1,0:T(8,128)}), f32[16,8,256]{2,1,0:T(8,128)S(1)}, u32[]{:S(2)}, u32[]{:S(2)}) async-start(f32[16,8,256]{2,1,0:T(8,128)} %convolution_bitcast_fusion.3), calls=%async_computation.5 | async-start | bytes 262144 | tf_op jit(solution)/shard_map/all_to_all | solution.py:38
  141.1 9.7 %all-to-all-start.6 = ((bf16[16,8,256]{2,1,0:T(8,128)(2,1)}), bf16[16,8,256]{2,1,0:T(8,128)(2,1)S(1)}, u32[]{:S(2)}, u32[]{:S(2)}) async-start(bf16[16,8,256]{2,1,0:T(8,128)(2,1)} %broadcast_in_dim.51), calls=%async_computation.6 | async-start | bytes 131072 | tf_op jit(solution)/shard_map/all_to_all | solution.py:22
  152.0 14.9 %all-to-all-start.7 = ((bf16[8,8,4096]{2,1,0:T(8,128)(2,1)}), bf16[8,8,4096]{2,1,0:T(8,128)(2,1)S(1)}, u32[]{:S(2)}, u32[]{:S(2)}) async-start(bf16[8,8,4096]{2,1,0:T(8,128)(2,1)} %broadcast_in_dim.53), calls=%async_computation.7 | async-start | bytes 1048576 | tf_op jit(solution)/shard_map/all_to_all | solution.py:22
  167.6 10.3 %all-to-all-start.9 = ((f32[16,8,128]{2,1,0:T(8,128)}), f32[16,8,128]{2,1,0:T(8,128)S(1)}, u32[]{:S(2)}, u32[]{:S(2)}) async-start(f32[16,8,128]{2,1,0:T(8,128)} %broadcast_in_dim.55), calls=%async_computation.9 | async-start | bytes 131072 | tf_op jit(solution)/shard_map/all_to_all | solution.py:22
  177.9 10.9 %all-to-all-start.8 = ((f32[8,8,1024]{2,1,0:T(8,128)}), f32[8,8,1024]{2,1,0:T(8,128)S(1)}, u32[]{:S(2)}, u32[]{:S(2)}) async-start(f32[8,8,1024]{2,1,0:T(8,128)} %fusion.47), calls=%async_computation.8 | async-start | bytes 524288 | tf_op jit(solution)/shard_map/all_to_all | solution.py:38
  211.4 9.8 %all-to-all-start.11 = ((f32[16,8,256]{2,1,0:T(8,128)}), f32[16,8,256]{2,1,0:T(8,128)S(1)}, u32[]{:S(2)}, u32[]{:S(2)}) async-start(f32[16,8,256]{2,1,0:T(8,128)} %convolution_bitcast_fusion.2), calls=%async_computation.11 | async-start | bytes 262144 | tf_op jit(solution)/shard_map/all_to_all | solution.py:38
  221.9 9.7 %all-to-all-start.12 = ((bf16[16,8,256]{2,1,0:T(8,128)(2,1)}), bf16[16,8,256]{2,1,0:T(8,128)(2,1)S(1)}, u32[]{:S(2)}, u32[]{:S(2)}) async-start(bf16[16,8,256]{2,1,0:T(8,128)(2,1)} %broadcast_in_dim.57), calls=%async_computation.12 | async-start | bytes 131072 | tf_op jit(solution)/shard_map/all_to_all | solution.py:22
  232.8 14.2 %all-to-all-start.13 = ((bf16[8,8,4096]{2,1,0:T(8,128)(2,1)}), bf16[8,8,4096]{2,1,0:T(8,128)(2,1)S(1)}, u32[]{:S(2)}, u32[]{:S(2)}) async-start(bf16[8,8,4096]{2,1,0:T(8,128)(2,1)} %broadcast_in_dim.59), calls=%async_computation.13 | async-start | bytes 1048576 | tf_op jit(solution)/shard_map/all_to_all | solution.py:22
  247.7 10.3 %all-to-all-start.15 = ((f32[16,8,128]{2,1,0:T(8,128)}), f32[16,8,128]{2,1,0:T(8,128)S(1)}, u32[]{:S(2)}, u32[]{:S(2)}) async-start(f32[16,8,128]{2,1,0:T(8,128)} %broadcast_in_dim.61), calls=%async_computation.15 | async-start | bytes 131072 | tf_op jit(solution)/shard_map/all_to_all | solution.py:22
  257.9 11.0 %all-to-all-start.14 = ((f32[8,8,1024]{2,1,0:T(8,128)}), f32[8,8,1024]{2,1,0:T(8,128)S(1)}, u32[]{:S(2)}, u32[]{:S(2)}) async-start(f32[8,8,1024]{2,1,0:T(8,128)} %fusion.45), calls=%async_computation.14 | async-start | bytes 524288 | tf_op jit(solution)/shard_map/all_to_all | solution.py:38
  292.1 9.8 %all-to-all-start.17 = ((f32[16,8,256]{2,1,0:T(8,128)}), f32[16,8,256]{2,1,0:T(8,128)S(1)}, u32[]{:S(2)}, u32[]{:S(2)}) async-start(f32[16,8,256]{2,1,0:T(8,128)} %convolution_bitcast_fusion.1), calls=%async_computation.17 | async-start | bytes 262144 | tf_op jit(solution)/shard_map/all_to_all | solution.py:38
  302.6 9.7 %all-to-all-start.18 = ((bf16[16,8,256]{2,1,0:T(8,128)(2,1)}), bf16[16,8,256]{2,1,0:T(8,128)(2,1)S(1)}, u32[]{:S(2)}, u32[]{:S(2)}) async-start(bf16[16,8,256]{2,1,0:T(8,128)(2,1)} %broadcast_in_dim.63), calls=%async_computation.18 | async-start | bytes 131072 | tf_op jit(solution)/shard_map/all_to_all | solution.py:22
  313.5 14.0 %all-to-all-start.19 = ((bf16[8,8,4096]{2,1,0:T(8,128)(2,1)}), bf16[8,8,4096]{2,1,0:T(8,128)(2,1)S(1)}, u32[]{:S(2)}, u32[]{:S(2)}) async-start(bf16[8,8,4096]{2,1,0:T(8,128)(2,1)} %broadcast_in_dim.65), calls=%async_computation.19 | async-start | bytes 1048576 | tf_op jit(solution)/shard_map/all_to_all | solution.py:22
  328.2 10.3 %all-to-all-start.21 = ((f32[16,8,128]{2,1,0:T(8,128)}), f32[16,8,128]{2,1,0:T(8,128)S(1)}, u32[]{:S(2)}, u32[]{:S(2)}) async-start(f32[16,8,128]{2,1,0:T(8,128)} %broadcast_in_dim.67), calls=%async_computation.21 | async-start | bytes 131072 | tf_op jit(solution)/shard_map/all_to_all | solution.py:22
  338.5 10.8 %all-to-all-start.20 = ((f32[8,8,1024]{2,1,0:T(8,128)}), f32[8,8,1024]{2,1,0:T(8,128)S(1)}, u32[]{:S(2)}, u32[]{:S(2)}) async-start(f32[8,8,1024]{2,1,0:T(8,128)} %fusion.43), calls=%async_computation.20 | async-start | bytes 524288 | tf_op jit(solution)/shard_map/all_to_all | solution.py:38
  (12 other events, 268.6 us)
Sparse Core Ops, SparseCore 0:
  10.6 86.6 all-gather.1
